TPU v7x, 16 devices: a whole 2x2x2 slice. The times are simulated.
16 devices in a mesh: dp: 1, tp: 16 (over x, y, z, core).
Axes of the slice: x: 2, y: 2, z: 2, core: 2. Of those that a mesh axis runs over, the one named last changes fastest.
Arguments:
- x: bfloat16 [2048, 3584], P('dp')
- dy: bfloat16 [2048, 3584], P('dp')
- gate: bfloat16 [2048, 14336], P('dp', 'tp')
- up: bfloat16 [2048, 14336], P('dp', 'tp')
- w_gate: bfloat16 [3584, 14336], P(None, 'tp')
- w_up: bfloat16 [3584, 14336], P(None, 'tp')
- w_down: bfloat16 [14336, 3584], P('tp')
Outputs:
- output 1: bfloat16 [2048, 3584], P('dp')
- output 2: bfloat16 [3584, 14336], P('dp', 'tp')
- output 3: bfloat16 [3584, 14336], P('dp', 'tp')
- output 4: bfloat16 [14336, 3584], P(('dp', 'tp'))
All inputs are finite; a program needn't handle non-finite values.
Results may differ from a plain program's by a relative error of at most 0.012.
Values are sent between devices in bfloat16 or wider.
A program may use at most 2 GiB of HBM per device.

v0:
```python
import jax
import jax.numpy as jnp
from jax import lax
from jax.sharding import PartitionSpec as P


def act(gate, up):
    return jax.nn.gelu(gate) * up


def solution(mesh):
    def step(x, dy, gate, up, w_gate, w_up, w_down):
        hidden, back = jax.vjp(act, gate.astype(jnp.float32), up.astype(jnp.float32))
        d_hidden = jnp.dot(dy, w_down.T, preferred_element_type=jnp.float32)
        d_gate, d_up = (g.astype(jnp.bfloat16) for g in back(d_hidden))
        term = jnp.dot(d_gate, w_gate.T, preferred_element_type=jnp.float32) + jnp.dot(d_up, w_up.T, preferred_element_type=jnp.float32)
        dx = lax.psum(term.astype(jnp.bfloat16), "tp")
        dw_gate = jnp.dot(x.T, d_gate, preferred_element_type=jnp.float32)
        dw_up = jnp.dot(x.T, d_up, preferred_element_type=jnp.float32)
        dw_down = jnp.dot(hidden.astype(jnp.bfloat16).T, dy, preferred_element_type=jnp.float32)
        return dx, *(g.astype(jnp.bfloat16) for g in (dw_gate, dw_up, dw_down))

    tokens, columns, rows = P("dp", None), P(None, "tp"), P("tp", None)
    return jax.shard_map(
        step,
        mesh=mesh,
        in_specs=(tokens, tokens, P("dp", "tp"), P("dp", "tp"), columns, columns, rows),
        out_specs=(tokens, P("dp", "tp"), P("dp", "tp"), P(("dp", "tp"), None)),
        check_vma=False,
    )
```

profile of v0, /device:TPU:0, one launch (start us, length us, event | category | flops | bytes accessed | tf_op | source)
XLA Modules:
  0.0 263.5 jit_solution(4230082221450964767)
XLA Ops:
  7.2 0.0 all-reduce.2.cloned.1.call-start
  7.2 0.0 copy-start
  7.2 25.9 %fusion.4 = (bf16[2048,896]{1,0:T(8,128)(2,1)S(1)}, f32[2048,896]{1,0:T(8,128)}) fusion(bf16[2048,896]{1,0:T(8,128)(2,1)} %param.9, bf16[2048,896]{1,0:T(8,128)(2,1)} %param.10, bf16[2048,3584]{1,0:T(8,128)(2,1)} %param.8, bf16[896,3584]{1,0:T(8,128)(2,1)} %param.13), kind=kOutput, calls=%fused_computation.12 | convolution fusion | flops 13195542528 | bytes 39452672 | tf_op jit(solution)/shard_map/dot_general | solution.py:14
  33.1 0.0 copy-start.1
  33.1 0.0 copy-done
  33.1 19.0 %fusion.21 = f32[2048,3584]{1,0:T(8,128)} fusion(bf16[2048,896]{1,0:T(8,128)(2,1)S(1)} %get-tuple-element.8, bf16[3584,896]{1,0:T(8,128)(2,1)S(1)} %copy-done), kind=kOutput, calls=%fused_computation.32 | convolution fusion | flops 13153337344 | bytes 39452672 | tf_op jit(solution)/shard_map/dot_general | solution.py:16
  52.1 0.0 copy-done.1
  52.1 25.9 %add_convert_fusion = bf16[2048,3584]{1,0:T(8,128)(2,1)} fusion(f32[2048,3584]{1,0:T(8,128)} %fusion.21, bf16[3584,896]{1,0:T(8,128)(2,1)} %param.12, f32[2048,896]{1,0:T(8,128)} %get-tuple-element.9, bf16[2048,896]{1,0:T(8,128)(2,1)} %param.9), kind=kOutput, calls=%fused_computation | convolution fusion | flops 13188202496 | bytes 61472768 | tf_op jit(solution)/shard_map/dot_general | solution.py:16
  78.0 0.0 all-reduce.2.cloned.1.call-update
  78.0 19.9 %fusion.10 = bf16[3584,896]{0,1:T(8,128)(2,1)} fusion(bf16[2048,896]{1,0:T(8,128)(2,1)} %copy-done.1, bf16[2048,3584]{1,0:T(8,128)(2,1)} %param.7), kind=kOutput, calls=%fused_computation.22 | convolution fusion | flops 13156548608 | bytes 24772608 | tf_op jit(solution)/shard_map/dot_general | solution.py:18
  97.9 9.6 %copy.11 = bf16[3584,896]{1,0:T(8,128)(2,1)} copy(bf16[3584,896]{0,1:T(8,128)(2,1)} %fusion.10) | data formatting | bytes 12845056
  107.5 25.1 %fusion.11 = bf16[3584,896]{0,1:T(8,128)(2,1)} fusion(bf16[2048,3584]{1,0:T(8,128)(2,1)} %param.7, f32[2048,896]{1,0:T(8,128)} %get-tuple-element.9, bf16[2048,896]{1,0:T(8,128)(2,1)} %param.9), kind=kOutput, calls=%fused_computation.23 | convolution fusion | flops 13176733696 | bytes 32112640 | tf_op jit(solution)/shard_map/dot_general | solution.py:19
  132.6 9.6 %copy.12 = bf16[3584,896]{1,0:T(8,128)(2,1)} copy(bf16[3584,896]{0,1:T(8,128)(2,1)} %fusion.11) | data formatting | bytes 12845056
  142.1 24.5 %convolution_convert_fusion = bf16[896,3584]{1,0:T(8,128)(2,1)} fusion(bf16[2048,3584]{1,0:T(8,128)(2,1)} %param.8, bf16[2048,896]{1,0:T(8,128)(2,1)} %param.10, bf16[2048,896]{1,0:T(8,128)(2,1)} %param.9), kind=kOutput, calls=%fused_computation.19 | convolution fusion | flops 13178568704 | bytes 28442624 | tf_op jit(solution)/shard_map/dot_general | solution.py:20
  166.6 76.9 %all-reduce.2.cloned.1.call-done = bf16[2048,3584]{1,0:T(8,128)(2,1)} async-done(((bf16[2048,3584]{1,0:T(8,128)(2,1)}), bf16[2048,3584]{1,0:T(8,128)(2,1)}) %all-reduce.2.cloned.1.call-update) | async-done | bytes 14680080 | tf_op jit(solution)/shard_map/psum | solution.py:17
  243.6 13.1 %copy.14 = bf16[2048,3584]{1,0:T(8,128)(2,1)} copy(bf16[2048,3584]{1,0:T(8,128)(2,1)} %all-reduce.2.cloned.1.call-done) | data formatting | bytes 29360128
Async XLA Ops:
  7.2 236.4 %all-reduce.2.cloned.1.call-start = ((), (), s32[]{:S(2)}) async-start(), calls=%async_computation | async-start | bytes 29360128 | tf_op jit(solution)/shard_map/psum | solution.py:17
  7.2 25.9 %copy-start = (bf16[3584,896]{1,0:T(8,128)(2,1)S(1)}, bf16[3584,896]{1,0:T(8,128)(2,1)}, u32[]{:S(2)}) copy-start(bf16[3584,896]{1,0:T(8,128)(2,1)} %param.11) | copy-start | bytes 19267588
  33.1 19.0 %copy-start.1 = (bf16[2048,896]{1,0:T(8,128)(2,1)}, bf16[2048,896]{1,0:T(8,128)(2,1)S(1)}, u32[]{:S(2)}) copy-start(bf16[2048,896]{1,0:T(8,128)(2,1)S(1)} %get-tuple-element.8) | copy-start | bytes 11010052
Sparse Core Ops, SparseCore 0:
  78.1 165.3 all-reduce.1
where the time goes:
time: 264 us
  matrix products  140 us (53%)
  waiting for transfers between devices  76.9 us (29%)
  local copies, waits for them, and re-layouts  32.2 us (12%)
  between operations  14 us (5%)
    psum x1, waiting for transfers between devices, step(): dx = lax.psum(term.astype(jnp.bfloat16), 'tp')  76.9 us
    unnamed x7, local copies, waits for them, and re-layouts  32.2 us
    dot_general x1, matrix products, step(): d_hidden = jnp.dot(dy, w_down.T, preferred_element_type=jnp.float32)  25.9 us
    dot_general x1, matrix products, step(): jnp.dot(d_up, w_up.T, preferred_element_type=jnp.float32)  25.9 us
    dot_general x1, matrix products, step(): dw_up = jnp.dot(x.T, d_up, preferred_element_type=jnp.float32)  25.1 us
    dot_general x1, matrix products, step(): jnp.dot(hidden.astype(jnp.bfloat16).T, dy, preferred_element_type=jnp.flo...  24.5 us
    dot_general x1, matrix products, step(): dw_gate = jnp.dot(x.T, d_gate, preferred_element_type=jnp.float32)  19.9 us
    dot_general x1, matrix products, step(): jnp.dot(d_gate, w_gate.T, preferred_element_type=jnp.float32)  19 us
  transfers between devices with their start and end apart: 1, of which 1 were waited for; matrix products, arithmetic and copies ran while one was open for 34% of the time, Pallas kernels for 0%

commit v1 on v0

v1 whole, which is shorter than its diff:
```python
import functools

import jax
import jax.numpy as jnp
from jax import lax
from jax.experimental import pallas as pl
from jax.experimental.pallas import tpu as pltpu
from jax.sharding import PartitionSpec as P

MESH = pl.DeviceIdType.MESH
BF, F32 = jnp.bfloat16, jnp.float32
CHUNK = 256
HALF = CHUNK // 2
TILE = 256
C0 = 0.7978845608028654
C1 = 0.044715
STRIDES = (8, 4, 2)
ORDERS = ((0, 1, 2), (1, 2, 0), (2, 0, 1))
NT = (((1,), (1,)), ((), ()))
TN = (((0,), (0,)), ((), ()))
NN = (((1,), (0,)), ((), ()))
D, RS1, RS2, RS3, AG3, AG2, AG1, DG = range(8)
ROWS_OF = (HALF, HALF // 2, HALF // 4, HALF // 8, HALF // 8, HALF // 4, HALF // 2, HALF)

EVENTS1 = {1: ((1, 1), (3, 3)), 2: ((7, 6), (6, 5)), 3: ((2, 2), (5, 4)), 5: ((4, 3),)}
EVENTS2 = {1: ((1, 1), (3, 3)), 2: ((7, 6), (6, 5)), 3: ((2, 2), (5, 4)), 4: ((4, 3),)}
LAST_LAG = 6


def kernel(x, dy, gate, up, w_gate, w_up, w_down, dx, dwg, dwu, dwd,
           wgu, wd, dgu, hidt, pbuf, own, summed, acc, r1, r2, r3,
           wsem, insem, colsem, outsem, lsem, ssem, rsem):
    rows, dim = x.shape
    ff = gate.shape[1]
    n_chunks = rows // CHUNK
    n_tiles = dim // TILE
    n_dx = 4
    dxw = dim // n_dx
    units = dim // 128
    w2 = units // 3
    w0 = units - 2 * w2
    parts = ((0, w0 * 128), (w0 * 128, w2 * 128), ((w0 + w2) * 128, w2 * 128))

    me = lax.axis_index("tp")
    core = me % 2
    bits = tuple((me // s) % 2 for s in STRIDES)
    near = tuple(me + s - 2 * s * b for s, b in zip(STRIDES, bits))
    partner = me + 1 - 2 * core

    def load_chunk(k, slot, dyb, gb, ub):
        r = pl.ds(pl.multiple_of(k * CHUNK, CHUNK), CHUNK)
        return (pltpu.make_async_copy(dy.at[r], dyb.at[slot], insem.at[0, slot]),
                pltpu.make_async_copy(gate.at[r], gb.at[slot], insem.at[1, slot]),
                pltpu.make_async_copy(up.at[r], ub.at[slot], insem.at[2, slot]))

    def load_col(t, q, xcol, dycol):
        c = pl.ds(pl.multiple_of(t * TILE, TILE), TILE)
        return (pltpu.make_async_copy(x.at[:, c], xcol.at[q], colsem.at[0, q]),
                pltpu.make_async_copy(dy.at[:, c], dycol.at[q], colsem.at[1, q]))

    wloads = (pltpu.make_async_copy(w_down, wd, wsem.at[0]),
              pltpu.make_async_copy(w_gate, wgu.at[:, 0:ff], wsem.at[1]),
              pltpu.make_async_copy(w_up, wgu.at[:, ff:2 * ff], wsem.at[2]))
    for c in wloads:
        c.start()

    barrier = pltpu.get_barrier_semaphore()
    for other in (*near, partner):
        pl.semaphore_signal(barrier, inc=1, device_id={"tp": other}, device_id_type=MESH)
    pl.semaphore_wait(barrier, 4)

    def send(src, dst, stage, k, to):
        pltpu.make_async_remote_copy(src_ref=src, dst_ref=dst, send_sem=ssem.at[stage, k], recv_sem=rsem.at[stage, k],
                                     device_id={"tp": to}, device_id_type=MESH).start()

    def await_bytes(stage, k, sems):
        ref = summed.at[0, 0:ROWS_OF[stage]]
        pltpu.make_async_copy(ref, ref, sems.at[stage, k]).wait()

    def geometry(p):
        c0, cw = parts[p]
        a, b, c = ORDERS[p]
        return slice(c0, c0 + cw), (bits[a], bits[b], bits[c]), (near[a], near[b], near[c])

    def at(o, n):
        return pl.ds(pl.multiple_of(o, HALF // 8), n)

    def stage0(k):
        send(pbuf.at[...], summed.at[k], D, k, partner)

    def stage1(k):
        await_bytes(D, k, ssem)
        await_bytes(D, k, rsem)
        h = HALF // 2
        a = lax.rem(k, 4)
        for p in range(3):
            cols, (b1, _, _), (to, _, _) = geometry(p)
            out, keep = at(h * (1 - b1), h), at(h * b1, h)
            summed[k, out, cols] = (own[out, cols] + summed[k, out, cols].astype(F32)).astype(BF)
            send(summed.at[k, out, cols], r1.at[k, :, cols], RS1, k, to)
            acc[a, :, cols] = own[keep, cols] + summed[k, keep, cols].astype(F32)

    def stage2(k):
        await_bytes(RS1, k, rsem)
        h = HALF // 4
        a = lax.rem(k, 4)
        for p in range(3):
            cols, (b1, b2, _), (_, to, _) = geometry(p)
            out, keep = at(h * (1 - b2), h), at(h * b2, h)
            stage = at(2 * h * b1 + h * (1 - b2), h)
            summed[k, stage, cols] = (acc[a, out, cols] + r1[k, out, cols].astype(F32)).astype(BF)
            send(summed.at[k, stage, cols], r2.at[k, :, cols], RS2, k, to)
            acc[a, keep, cols] = acc[a, keep, cols] + r1[k, keep, cols].astype(F32)

    def stage3(k):
        await_bytes(RS2, k, rsem)
        h = HALF // 8
        a = lax.rem(k, 4)
        for p in range(3):
            cols, (b1, b2, b3), (_, _, to) = geometry(p)
            out, keep = at(h * (1 - b3), h), at(h * b3, h)
            aout, akeep = at(2 * h * b2 + h * (1 - b3), h), at(2 * h * b2 + h * b3, h)
            stage = at(4 * h * b1 + 2 * h * b2 + h * (1 - b3), h)
            summed[k, stage, cols] = (acc[a, aout, cols] + r2[k, out, cols].astype(F32)).astype(BF)
            send(summed.at[k, stage, cols], r3.at[k, :, cols], RS3, k, to)
            acc[a, akeep, cols] = acc[a, akeep, cols] + r2[k, keep, cols].astype(F32)

    def stage4(k):
        await_bytes(RS3, k, rsem)
        h = HALF // 8
        a = lax.rem(k, 4)
        for p in range(3):
            cols, (b1, b2, b3), (_, _, to) = geometry(p)
            akeep = at(2 * h * b2 + h * b3, h)
            o = 4 * h * b1 + 2 * h * b2 + h * b3
            mine = at(o, h)
            place = at(k * CHUNK + core * HALF + o, h)
            summed[k, mine, cols] = (acc[a, akeep, cols] + r3[k, :, cols].astype(F32)).astype(BF)
            send(summed.at[k, mine, cols], dx.at[place, cols], AG3, k, to)
            pltpu.make_async_copy(summed.at[k, mine, cols], dx.at[place, cols], lsem.at[k]).start()

    def gather(k, got, stage, span, which):
        await_bytes(got, k, rsem)
        for p in range(3):
            cols, (b1, b2, _), tos = geometry(p)
            o = (HALF // 2) * b1 + (HALF // 4) * b2 if which == 1 else (HALF // 2) * b1
            place = at(k * CHUNK + core * HALF + o, span)
            send(dx.at[place, cols], dx.at[place, cols], stage, k, tos[which])

    def stage5(k):
        ref = summed.at[0, 0:HALF // 8]
        pltpu.make_async_copy(ref, ref, lsem.at[k]).wait()
        gather(k, AG3, AG2, HALF // 4, 1)

    def stage6(k):
        gather(k, AG2, AG1, HALF // 2, 0)

    def stage7(k):
        await_bytes(AG1, k, rsem)
        place = at(k * CHUNK + core * HALF, HALF)
        send(dx.at[place], dx.at[place], DG, k, partner)

    stages = (stage0, stage1, stage2, stage3, stage4, stage5, stage6, stage7)

    def run(table, s, j):
        for stage, lag in table.get(j, ()):
            k = s - lag

            @pl.when(jnp.logical_and(k >= 0, k < n_chunks))
            def _():
                stages[stage](k)

    def slot1(bufs, s):
        dyb, gb, ub = bufs
        q = lax.rem(s, 2)

        @pl.when(s + 1 < n_chunks)
        def _():
            for c in load_chunk(s + 1, 1 - q, *bufs):
                c.start()

        for c in load_chunk(s, q, *bufs):
            c.wait()

        @pl.when(s == 0)
        def _():
            wloads[0].wait()

        base = pl.multiple_of(s * CHUNK, CHUNK)
        dh = lax.dot_general(dyb[q], wd[...], NT, preferred_element_type=F32)
        g, u = gb[q].astype(F32), ub[q].astype(F32)
        g2 = g * g
        t = jnp.tanh((C0 * g) * (1.0 + C1 * g2))
        cdf = 0.5 + 0.5 * t
        gelu = g * cdf
        slope = cdf + g * (cdf * (1.0 - t)) * (C0 + (3.0 * C0 * C1) * g2)
        hidt[:, pl.ds(base, CHUNK)] = (gelu * u).astype(BF).T
        dgu[pl.ds(base, CHUNK), 0:ff] = (dh * u * slope).astype(BF)
        dgu[pl.ds(base, CHUNK), ff:2 * ff] = (dh * gelu).astype(BF)

        @pl.when(s == 0)
        def _():
            wloads[1].wait()
            wloads[2].wait()

        run(EVENTS1, s, 1)
        theirs = pl.ds(pl.multiple_of(base + HALF * (1 - core), HALF), HALF)
        mine = pl.ds(pl.multiple_of(base + HALF * core, HALF), HALF)
        for n in range(n_dx):
            cols = slice(n * dxw, (n + 1) * dxw)
            lhs = jnp.concatenate([dgu[theirs], dgu[mine]], axis=0)
            term = lax.dot_general(lhs, wgu[cols], NT, preferred_element_type=F32)
            pbuf[:, cols] = term[:HALF].astype(BF)
            own[:, cols] = term[HALF:]
            if n == n_dx - 1:
                stage0(s)
            run(EVENTS1, s, n + 2)

    def phase1(*bufs):
        for c in load_chunk(0, 0, *bufs):
            c.start()

        def body(s, _):
            slot1(bufs, s)
            return ()

        lax.fori_loop(0, n_chunks, body, ())

    pl.run_scoped(phase1, pltpu.VMEM((2, CHUNK, dim), BF), pltpu.VMEM((2, CHUNK, ff), BF), pltpu.VMEM((2, CHUNK, ff), BF))

    def put(t, q, outg, outd):
        r = pl.ds(pl.multiple_of(t * TILE, TILE), TILE)
        return (pltpu.make_async_copy(outg.at[q, :, 0:ff], dwg.at[r], outsem.at[0, q]),
                pltpu.make_async_copy(outg.at[q, :, ff:2 * ff], dwu.at[r], outsem.at[1, q]),
                pltpu.make_async_copy(outd.at[q], dwd.at[:, r], outsem.at[2, q]))

    def slot2(bufs, i):
        xcol, dycol, outg, outd = bufs
        s = n_chunks + i
        for q in range(2):
            tile = 2 * i + q
            loads, puts = load_col(tile, q, xcol, dycol), put(tile, q, outg, outd)
            for c in loads:
                c.wait()

            @pl.when(i > 0)
            def _():
                for c in puts:
                    c.wait()

            outg[q] = lax.dot_general(xcol[q], dgu[...], TN, preferred_element_type=F32).astype(BF)
            puts[0].start()
            puts[1].start()
            run(EVENTS2, s, 2 * q + 1)
            outd[q] = lax.dot_general(hidt[...], dycol[q], NN, preferred_element_type=F32).astype(BF)
            puts[2].start()

            @pl.when(tile + 2 < n_tiles)
            def _():
                for c in load_col(tile + 2, q, xcol, dycol):
                    c.start()

            run(EVENTS2, s, 2 * q + 2)

    n_slots = n_tiles // 2

    def phase2(*bufs):
        for q in range(2):
            for c in load_col(q, q, *bufs[:2]):
                c.start()

        def body(i, _):
            slot2(bufs, i)
            return ()

        lax.fori_loop(0, n_slots, body, ())
        for q in range(2):
            for c in put(0, q, *bufs[2:]):
                c.wait()

    pl.run_scoped(phase2, pltpu.VMEM((2, rows, TILE), BF), pltpu.VMEM((2, rows, TILE), BF),
                  pltpu.VMEM((2, TILE, 2 * ff), BF), pltpu.VMEM((2, ff, TILE), BF))

    def slot3(s, _):
        for j in range(1, 6):
            run(EVENTS1, s, j)
        return ()

    lax.fori_loop(n_chunks + n_slots, max(n_chunks + n_slots, n_chunks + LAST_LAG), slot3, ())

    def finish(k, _):
        await_bytes(DG, k, rsem)
        for stage in range(RS1, DG + 1):
            await_bytes(stage, k, ssem)
        return ()

    lax.fori_loop(0, n_chunks, finish, ())


def backward(x, dy, gate, up, w_gate, w_up, w_down):
    rows, dim = x.shape
    ff = gate.shape[1]
    n_chunks = rows // CHUNK
    anyspec = pl.BlockSpec(memory_space=pl.ANY)
    vmem = pltpu.VMEM
    return pl.pallas_call(
        kernel,
        out_shape=(jax.ShapeDtypeStruct((rows, dim), BF), jax.ShapeDtypeStruct((dim, ff), BF),
                   jax.ShapeDtypeStruct((dim, ff), BF), jax.ShapeDtypeStruct((ff, dim), BF)),
        in_specs=[anyspec] * 7,
        out_specs=(anyspec,) * 4,
        scratch_shapes=[
            vmem((dim, 2 * ff), BF), vmem((ff, dim), BF), vmem((rows, 2 * ff), BF), vmem((ff, rows), BF),
            vmem((HALF, dim), BF), vmem((HALF, dim), F32), vmem((n_chunks, HALF, dim), BF), vmem((4, HALF // 2, dim), F32),
            vmem((n_chunks, HALF // 2, dim), BF), vmem((n_chunks, HALF // 4, dim), BF), vmem((n_chunks, HALF // 8, dim), BF),
            pltpu.SemaphoreType.DMA((3,)), pltpu.SemaphoreType.DMA((3, 2)), pltpu.SemaphoreType.DMA((2, 2)),
            pltpu.SemaphoreType.DMA((3, 2)), pltpu.SemaphoreType.DMA((n_chunks,)),
            pltpu.SemaphoreType.DMA((8, n_chunks)), pltpu.SemaphoreType.DMA((8, n_chunks)),
        ],
        compiler_params=pltpu.CompilerParams(collective_id=0, has_side_effects=True, vmem_limit_bytes=67_000_000),
        name="mlp_backward",
    )(x, dy, gate, up, w_gate, w_up, w_down)


def solution(mesh):
    tokens, columns, rows = P("dp", None), P(None, "tp"), P("tp", None)
    return jax.shard_map(
        backward,
        mesh=mesh,
        in_specs=(tokens, tokens, P("dp", "tp"), P("dp", "tp"), columns, columns, rows),
        out_specs=(tokens, P("dp", "tp"), P("dp", "tp"), P(("dp", "tp"), None)),
        check_vma=False,
    )
```

time: 264 us -> 180 us (0.68)
  Pallas kernels: 0 us -> 152 us
  matrix products: 140 us -> 0 us
  waiting for transfers between devices: 76.9 us -> 0 us
  between operations: 14 us -> 0.65 us
  local copies, waits for them, and re-layouts: 32.2 us -> 27.2 us
    pallas_call x0 -> x1, Pallas kernels: none -> 152 us  [backward(): pl.pallas_call(kernel, out_shape=(jax.ShapeDtypeStruct((rows, dim), BF),...]
    dot_general x6 -> x0, matrix products: 140 us -> none  [the longest x1 25.9 us: step(): d_hidden = jnp.dot(dy, w_down.T, preferred_element_type=jnp.float32)]
    psum x1 -> x0, waiting for transfers between devices: 76.9 us -> none  [step(): dx = lax.psum(term.astype(jnp.bfloat16), 'tp')]
    unnamed x7 -> x10, local copies, waits for them, and re-layouts: 32.2 us -> 27.2 us
  transfers between devices with their start and end apart: 1 -> 0, of which waited for: 1 -> 0; matrix products, arithmetic and copies ran while one was open for 34% -> 0% of each run, Pallas kernels for 0% -> 0%
where the time goes in v1:
time: 180 us
  Pallas kernels  152 us (84%)
  local copies, waits for them, and re-layouts  27.2 us (15%)
    pallas_call x1, Pallas kernels, backward(): pl.pallas_call(kernel, out_shape=(jax.ShapeDtypeStruct((rows, dim), BF),...  152 us
    unnamed x10, local copies, waits for them, and re-layouts  27.2 us

profile of v1, /device:TPU:0, one launch (start us, length us, event | category | flops | bytes accessed | tf_op | source)
XLA Modules:
  0.0 179.6 jit_solution(10956819936974197349)
XLA Ops:
  0.6 151.8 %mlp_backward.1 = (bf16[2048,3584]{1,0:T(8,128)(2,1)}, bf16[3584,896]{1,0:T(8,128)(2,1)}, bf16[3584,896]{1,0:T(8,128)(2,1)}, bf16[896,3584]{1,0:T(8,128)(2,1)}) custom-call(bf16[2048,3584]{1,0:T(8,128)(2,1)} %x.1, bf16[2048,3584]{1,0:T(8,128)(2,1)} %dy.1, bf16[2048,896]{1,0:T(8,128)(2,1)} %gate.1, bf16[2048,896]{1,0:T(8,128)(2,1)} %up.1, ...), custom_call_target="tpu_custom_call" | custom-call | tf_op jit(solution)/shard_map/mlp_backward/pallas_call | solution.py:306
  152.4 13.1 %copy.15 = bf16[2048,3584]{1,0:T(8,128)(2,1)} copy(bf16[2048,3584]{1,0:T(8,128)(2,1)} %get-tuple-element.8) | data formatting | bytes 29360128
  165.5 0.0 copy-start
  165.5 0.0 slice-start
  165.5 6.7 %copy.16 = bf16[3584,896]{1,0:T(8,128)(2,1)} copy(bf16[3584,896]{1,0:T(8,128)(2,1)} %get-tuple-element.9) | data formatting | bytes 12845056
  172.3 0.0 copy-done
  172.3 0.0 slice-start.1
  172.3 3.3 %copy.17 = bf16[3584,896]{1,0:T(8,128)(2,1)} copy(bf16[3584,896]{1,0:T(8,128)(2,1)S(1)} %copy-done) | data formatting | bytes 12845056
  175.5 0.0 slice-done
  175.5 1.3 slice-done.1
  176.9 2.7 %copy.18 = bf16[896,3584]{1,0:T(8,128)(2,1)} copy(bf16[896,3584]{1,0:T(8,128)(2,1)S(1)} %bitcast.1) | data formatting | bytes 12845056
  (1 shorter events, 0.0 us)
Async XLA Ops:
  165.5 6.8 %copy-start = (bf16[3584,896]{1,0:T(8,128)(2,1)S(1)}, bf16[3584,896]{1,0:T(8,128)(2,1)}, u32[]{:S(2)}) copy-start(bf16[3584,896]{1,0:T(8,128)(2,1)} %get-tuple-element.10) | copy-start | bytes 19267588
  165.5 10.0 %slice-start = ((s8[6422528]{0:T(1024)(128)(4,1)}), s8[4194304]{0:T(1024)(128)(4,1)S(1)}, s32[]{:S(2)}) async-start(s8[6422528]{0:T(1024)(128)(4,1)} %bitcast), calls=%async_computation | async-start | bytes 8388608
  172.3 4.6 %slice-start.1 = ((s8[6422528]{0:T(1024)(128)(4,1)}), s8[2228224]{0:T(1024)(128)(4,1)S(1)}, s32[]{:S(2)}) async-start(s8[6422528]{0:T(1024)(128)(4,1)} %bitcast), calls=%async_computation.1 | async-start | bytes 4456448

commit v2 on v0

v2 whole, which is shorter than its diff:
```python
import functools

import jax
import jax.numpy as jnp
from jax import lax
from jax.experimental import pallas as pl
from jax.experimental.pallas import tpu as pltpu
from jax.sharding import PartitionSpec as P

MESH = pl.DeviceIdType.MESH
BF, F32 = jnp.bfloat16, jnp.float32
CHUNK = 256
HALF = CHUNK // 2
SLOTS = 4
VMEM_LIMIT, WRITER_LIMIT = 32_000_000, 1_000_000
TILE = 256
C0 = 0.7978845608028654
C1 = 0.044715
STRIDES = (8, 4, 2)
NT = (((1,), (1,)), ((), ()))
TN = (((0,), (0,)), ((), ()))
NN = (((1,), (0,)), ((), ()))
D, RS1, RS2, RS3, AG3, AG2, AG1, DG = range(8)
ROWS_OF = (HALF, HALF // 2, HALF // 4, HALF // 8, HALF // 8, HALF // 4, HALF // 2, HALF)

POINTS = (
    (2, 4, 6, 8, 10, 12, 14, 16),
    (4, 7, 8, 11, 12, 15, 18, 19),
    (6, 9, 10, 14, 17, 18, 20, 21),
    (7, 11, 12, 16, 20, 21, 22, 23),
    (9, 13, 14, 18, 22, 23, 24, 25),
    (11, 20, 22, 25, 26, 27, 28, 30),
    (14, 23, 25, 28, 29, 31, 32, 33),
)
PRIO = (4, 3, 2, 5, 1, 7, 6)


def kernel(x, dy, gate, up, w_gate, w_up, w_down, kept, dgu, hidt, pbuf, own, staged, acc,
           wsem, insem, colsem, credit, ssem, rsem):
    rows, dim = x.shape
    ff = gate.shape[1]
    n_chunks = rows // CHUNK
    n_tiles = dim // TILE
    n_blocks = dim // ff
    down = slice(rows, rows + ff)
    starts = (rows + ff, rows + 2 * ff)

    units = dim // 128
    w2 = units // 3
    w0 = units - 2 * w2
    parts = ((0, w0 * 128), (w0 * 128, w2 * 128), ((w0 + w2) * 128, w2 * 128))

    me = lax.axis_index("tp")
    core = me % 2
    bits = tuple((me // s) % 2 for s in STRIDES)
    near = tuple(me + s - 2 * s * b for s, b in zip(STRIDES, bits))
    partner = me + 1 - 2 * core

    def load_chunk(k, slot, dyb, gb, ub):
        r = pl.ds(pl.multiple_of(k * CHUNK, CHUNK), CHUNK)
        return (pltpu.make_async_copy(dy.at[r], dyb.at[slot], insem.at[0, slot]),
                pltpu.make_async_copy(gate.at[r], gb.at[slot], insem.at[1, slot]),
                pltpu.make_async_copy(up.at[r], ub.at[slot], insem.at[2, slot]))

    def load_col(t, q, xcol, dycol):
        c = pl.ds(pl.multiple_of(t * TILE, TILE), TILE)
        return (pltpu.make_async_copy(x.at[:, c], xcol.at[q], colsem.at[0, q]),
                pltpu.make_async_copy(dy.at[:, c], dycol.at[q], colsem.at[1, q]))

    def block(w, b):
        return slice(starts[w], starts[w] + ff), slice(b * ff, (b + 1) * ff)

    def weight(w, lo, hi):
        pieces = []
        while lo < hi:
            b = lo // ff
            end = min(hi, (b + 1) * ff)
            pieces.append(kept[starts[w] + lo - b * ff:starts[w] + end - b * ff, b * ff:(b + 1) * ff])
            lo = end
        return jnp.concatenate(pieces, axis=0)

    download = pltpu.make_async_copy(w_down, kept.at[down], wsem.at[2 * n_blocks])
    wloads = tuple(tuple(pltpu.make_async_copy(src.at[b * ff:(b + 1) * ff], kept.at[block(w, b)], wsem.at[2 * b + w])
                         for w, src in enumerate((w_gate, w_up))) for b in range(n_blocks))
    download.start()

    barrier = pltpu.get_barrier_semaphore()
    for other in (*near, partner):
        pl.semaphore_signal(barrier, inc=1, device_id={"tp": other}, device_id_type=MESH)
    pl.semaphore_wait(barrier, 4)

    def send(src, dst, stage, k, to):
        pltpu.make_async_remote_copy(src_ref=src, dst_ref=dst, send_sem=ssem.at[stage, k], recv_sem=rsem.at[stage, k],
                                     device_id={"tp": to}, device_id_type=MESH).start()

    def await_bytes(stage, k, sems):
        ref = kept.at[0:ROWS_OF[stage]]
        pltpu.make_async_copy(ref, ref, sems.at[stage, k]).wait()

    def pick(values, i):
        return jnp.where(i == 0, values[0], jnp.where(i == 1, values[1], values[2]))

    def geometry(p, k):
        c0, cw = parts[p]
        dims = [lax.rem(p + k + i, 3) for i in range(3)]
        return slice(c0, c0 + cw), [pick(bits, d) for d in dims], [pick(near, d) for d in dims]

    def at(o, n):
        return pl.ds(pl.multiple_of(o, HALF // 8), n)

    def mine_at(k, o, n):
        return at(k * CHUNK + HALF * core + o, n)

    def spare_at(k, o, n):
        return at(k * CHUNK + HALF * (1 - core) + o, n)

    def stage0(k):
        send(pbuf, kept.at[spare_at(k, 0, HALF)], D, k, partner)

    q1, q2, q3 = HALF // 2, HALF // 4, HALF // 8

    def stage1(k):
        await_bytes(D, k, ssem)
        await_bytes(D, k, rsem)

        @pl.when(k >= SLOTS)
        def _():
            for stage in (RS1, RS2, RS3):
                await_bytes(stage, k - SLOTS, ssem)

        a = lax.rem(k, SLOTS)
        for p in range(3):
            cols, (b1, _, _), (to, _, _) = geometry(p, k)
            out, keep = q1 * (1 - b1), q1 * b1
            staged[a, 0:q1, cols] = (own[at(out, q1), cols] + kept[mine_at(k, out, q1), cols].astype(F32)).astype(BF)
            send(staged.at[a, 0:q1, cols], kept.at[spare_at(k, 0, q1), cols], RS1, k, to)
            acc[a, :, cols] = own[at(keep, q1), cols] + kept[mine_at(k, keep, q1), cols].astype(F32)

    def stage2(k):
        await_bytes(RS1, k, rsem)
        a = lax.rem(k, SLOTS)
        for p in range(3):
            cols, (_, b2, _), (_, to, _) = geometry(p, k)
            out, keep = q2 * (1 - b2), q2 * b2
            stage = slice(q1, q1 + q2)
            staged[a, stage, cols] = (acc[a, at(out, q2), cols] + kept[spare_at(k, out, q2), cols].astype(F32)).astype(BF)
            send(staged.at[a, stage, cols], kept.at[spare_at(k, q1, q2), cols], RS2, k, to)
            acc[a, at(keep, q2), cols] = acc[a, at(keep, q2), cols] + kept[spare_at(k, keep, q2), cols].astype(F32)

    def stage3(k):
        await_bytes(RS2, k, rsem)
        a = lax.rem(k, SLOTS)
        for p in range(3):
            cols, (_, b2, b3), (_, _, to) = geometry(p, k)
            out, keep = q3 * (1 - b3), q3 * b3
            stage = slice(q1 + q2, q1 + q2 + q3)
            staged[a, stage, cols] = (acc[a, at(q2 * b2 + out, q3), cols]
                                      + kept[spare_at(k, q1 + out, q3), cols].astype(F32)).astype(BF)
            send(staged.at[a, stage, cols], kept.at[spare_at(k, q1 + q2, q3), cols], RS3, k, to)
            place = at(q2 * b2 + keep, q3)
            acc[a, place, cols] = acc[a, place, cols] + kept[spare_at(k, q1 + keep, q3), cols].astype(F32)

    def stage4(k):
        await_bytes(RS3, k, rsem)
        a = lax.rem(k, SLOTS)
        for p in range(3):
            cols, (b1, b2, b3), (_, _, to) = geometry(p, k)
            place = mine_at(k, q1 * b1 + q2 * b2 + q3 * b3, q3)
            kept[place, cols] = (acc[a, at(q2 * b2 + q3 * b3, q3), cols]
                                 + kept[spare_at(k, q1 + q2, q3), cols].astype(F32)).astype(BF)
            send(kept.at[place, cols], kept.at[place, cols], AG3, k, to)
        pl.semaphore_signal(credit, inc=1, device_id={"tp": partner}, device_id_type=MESH)

    def gather(k, got, stage, span, which):
        await_bytes(got, k, rsem)
        for p in range(3):
            cols, (b1, b2, _), tos = geometry(p, k)
            place = mine_at(k, q1 * b1 + q2 * b2 if which == 1 else q1 * b1, span)
            send(kept.at[place, cols], kept.at[place, cols], stage, k, tos[which])

    def stage5(k):
        gather(k, AG3, AG2, q2, 1)

    def stage6(k):
        gather(k, AG2, AG1, q1, 0)

    def stage7(k):
        await_bytes(AG1, k, rsem)
        pl.semaphore_wait(credit, 1)
        place = mine_at(k, 0, HALF)
        send(kept.at[place], kept.at[place], DG, k, partner)

    stages = (stage0, stage1, stage2, stage3, stage4, stage5, stage6, stage7)

    def run(base, n, per, i, j):
        for stage in PRIO:
            turns = [(k, (p - base) // per) for k, p in enumerate(POINTS[stage - 1])
                     if base <= p < base + n * per and (p - base) % per == j]
            if turns:
                k = sum(jnp.where(i == t, k, 0) for k, t in turns)
                now = functools.reduce(jnp.logical_or, [i == t for _, t in turns])

                @pl.when(now)
                def _():
                    stages[stage](k)

    def slot1(bufs, s):
        dyb, gb, ub = bufs
        q = lax.rem(s, 2)

        @pl.when(s + 1 < n_chunks)
        def _():
            for c in load_chunk(s + 1, 1 - q, *bufs):
                c.start()

        @pl.when(s == 0)
        def _():
            download.wait()
            for pair in wloads:
                for c in pair:
                    c.start()

        for c in load_chunk(s, q, *bufs):
            c.wait()

        base = pl.multiple_of(s * CHUNK, CHUNK)
        dh = lax.dot_general(dyb[q], kept[down], NT, preferred_element_type=F32)
        g, u = gb[q].astype(F32), ub[q].astype(F32)
        g2 = g * g
        t = jnp.tanh((C0 * g) * (1.0 + C1 * g2))
        cdf = 0.5 + 0.5 * t
        gelu = g * cdf
        slope = cdf + g * (cdf * (1.0 - t)) * (C0 + (3.0 * C0 * C1) * g2)
        hidt[:, pl.ds(base, CHUNK)] = (gelu * u).astype(BF).T
        dgu[pl.ds(base, CHUNK), 0:ff] = (dh * u * slope).astype(BF)
        dgu[pl.ds(base, CHUNK), ff:2 * ff] = (dh * gelu).astype(BF)

        @pl.when(s == 0)
        def _():
            for pair in wloads:
                for c in pair:
                    c.wait()

        run(0, n_chunks, 2, s, 0)
        theirs = pl.ds(pl.multiple_of(base + HALF * (1 - core), HALF), HALF)
        mine = pl.ds(pl.multiple_of(base + HALF * core, HALF), HALF)
        lhs = jnp.concatenate([dgu[theirs], dgu[mine]], axis=0)
        for n in range(2):
            cols = slice(n * (dim // 2), (n + 1) * (dim // 2))
            rhs = jnp.concatenate([weight(w, cols.start, cols.stop) for w in range(2)], axis=1)
            term = lax.dot_general(lhs, rhs, NT, preferred_element_type=F32)
            pbuf[:, cols] = term[:HALF].astype(BF)
            own[:, cols] = term[HALF:]
        stage0(s)
        run(0, n_chunks, 2, s, 1)

    def phase1(*bufs):
        for c in load_chunk(0, 0, *bufs):
            c.start()

        def body(s, _):
            slot1(bufs, s)
            return ()

        lax.fori_loop(0, n_chunks, body, ())

    pl.run_scoped(phase1, pltpu.VMEM((2, CHUNK, dim), BF), pltpu.VMEM((2, CHUNK, ff), BF), pltpu.VMEM((2, CHUNK, ff), BF))

    base2 = n_chunks * 2

    def slot2(bufs, t):
        q = lax.rem(t, 3)

        @pl.when(t + 2 < n_tiles)
        def _():
            for c in load_col(t + 2, lax.rem(t + 2, 3), *bufs):
                c.start()

        xcol, dycol = bufs
        loads = load_col(t, q, *bufs)
        r = pl.ds(pl.multiple_of(t * TILE, TILE), TILE)
        loads[0].wait()
        loads[1].wait()
        dw = lax.dot_general(xcol[q], dgu[...], TN, preferred_element_type=F32)
        dw = dw.astype(BF)
        for i in range(TILE // 128):
            row = t * TILE + i * 128
            lanes = pl.ds(pl.multiple_of((row // ff) * ff, 128), ff)
            for w in range(2):
                place = pl.ds(pl.multiple_of(starts[w] + row % ff, 128), 128)
                kept[place, lanes] = dw[i * 128:(i + 1) * 128, w * ff:(w + 1) * ff]
        kept[down, r] = lax.dot_general(hidt[...], dycol[q], NN, preferred_element_type=F32).astype(BF)
        run(base2, n_tiles, 1, t, 0)

    def phase2(*bufs):
        for t in range(2):
            for c in load_col(t, t, *bufs):
                c.start()

        def body(t, _):
            slot2(bufs, t)
            return ()

        lax.fori_loop(0, n_tiles, body, ())

    pl.run_scoped(phase2, pltpu.VMEM((3, rows, TILE), BF), pltpu.VMEM((3, rows, TILE), BF))

    rest = sorted((p, PRIO.index(stage), stage, k) for stage in range(1, 8) for k, p in enumerate(POINTS[stage - 1])
                  if p >= base2 + n_tiles)
    for _, _, stage, k in rest:
        stages[stage](k)

    def finish(k, _):
        await_bytes(DG, k, rsem)
        for stage in (AG3, AG2, AG1, DG):
            await_bytes(stage, k, ssem)

        @pl.when(k >= n_chunks - SLOTS)
        def _():
            for stage in (RS1, RS2, RS3):
                await_bytes(stage, k, ssem)

        return ()

    lax.fori_loop(0, n_chunks, finish, ())


def writer(kept, dx, dwg, dwu, dwd, sem):
    rows, (dim, ff) = dx.shape[0], dwg.shape
    pairs = [(kept.at[0:rows], dx), (kept.at[rows:rows + ff], dwd)]
    for w, out in enumerate((dwg, dwu)):
        start = rows + (1 + w) * ff
        pairs += [(kept.at[start:start + ff, b * ff:(b + 1) * ff], out.at[b * ff:(b + 1) * ff]) for b in range(dim // ff)]
    copies = [pltpu.make_async_copy(a, b, sem.at[i]) for i, (a, b) in enumerate(pairs)]
    for c in copies:
        c.start()
    for c in copies:
        c.wait()


def backward(x, dy, gate, up, w_gate, w_up, w_down):
    rows, dim = x.shape
    ff = gate.shape[1]
    n_chunks, n_blocks = rows // CHUNK, dim // ff
    hbm, inside = pl.BlockSpec(memory_space=pl.ANY), pl.BlockSpec(memory_space=pltpu.VMEM)
    vmem, dma = pltpu.VMEM, pltpu.SemaphoreType.DMA
    kept = pl.pallas_call(
        kernel,
        out_shape=vmem((rows + 3 * ff, dim), BF),
        in_specs=[hbm] * 7,
        out_specs=inside,
        scratch_shapes=[
            vmem((rows, 2 * ff), BF), vmem((ff, rows), BF), vmem((HALF, dim), BF), vmem((HALF, dim), F32),
            vmem((SLOTS, HALF // 8 * 7, dim), BF), vmem((SLOTS, HALF // 2, dim), F32),
            dma((2 * n_blocks + 1,)), dma((3, 2)), dma((2, 3)), pltpu.SemaphoreType.REGULAR,
            dma((8, n_chunks)), dma((8, n_chunks)),
        ],
        compiler_params=pltpu.CompilerParams(collective_id=0, has_side_effects=True, vmem_limit_bytes=VMEM_LIMIT),
        name="mlp_backward",
    )(x, dy, gate, up, w_gate, w_up, w_down)
    return pl.pallas_call(
        writer,
        out_shape=tuple(jax.ShapeDtypeStruct(g, BF) for g in ((rows, dim), (dim, ff), (dim, ff), (ff, dim))),
        in_specs=[inside],
        out_specs=(hbm,) * 4,
        scratch_shapes=[dma((2 * n_blocks + 2,))],
        compiler_params=pltpu.CompilerParams(vmem_limit_bytes=WRITER_LIMIT),
        name="writer",
    )(kept)


def solution(mesh):
    tokens, columns, rows = P("dp", None), P(None, "tp"), P("tp", None)
    return jax.shard_map(
        backward,
        mesh=mesh,
        in_specs=(tokens, tokens, P("dp", "tp"), P("dp", "tp"), columns, columns, rows),
        out_specs=(tokens, P("dp", "tp"), P("dp", "tp"), P(("dp", "tp"), None)),
        check_vma=False,
    )
```

time: 264 us -> 132 us (0.50)
  matrix products: 140 us -> 0 us
  Pallas kernels: 0 us -> 131 us
  waiting for transfers between devices: 76.9 us -> 0 us
  local copies, waits for them, and re-layouts: 32.2 us -> 0 us
  between operations: 14 us -> 0.64 us
    dot_general x6 -> x0, matrix products: 140 us -> none  [the longest x1 25.9 us: step(): d_hidden = jnp.dot(dy, w_down.T, preferred_element_type=jnp.float32)]
    pallas_call x0 -> x2, Pallas kernels: none -> 131 us  [the longest x1 119 us: backward(): pl.pallas_call(kernel, out_shape=vmem((rows + 3 * ff, dim), BF), in_specs...]
    psum x1 -> x0, waiting for transfers between devices: 76.9 us -> none  [step(): dx = lax.psum(term.astype(jnp.bfloat16), 'tp')]
    unnamed x7 -> x0, local copies, waits for them, and re-layouts: 32.2 us -> none
  transfers between devices with their start and end apart: 1 -> 0, of which waited for: 1 -> 0; matrix products, arithmetic and copies ran while one was open for 34% -> 0% of each run, Pallas kernels for 0% -> 0%
where the time goes in v2:
time: 132 us; the launch traced here: 131 us
  Pallas kernels  131 us (99%)
    pallas_call x1, Pallas kernels, backward(): pl.pallas_call(kernel, out_shape=vmem((rows + 3 * ff, dim), BF), in_specs...  119 us
    pallas_call x1, Pallas kernels, backward(): pl.pallas_call(writer, out_shape=tuple((jax.ShapeDtypeStruct(g, BF) for g...  11.4 us

profile of v2, /device:TPU:0, one launch (start us, length us, event | category | flops | bytes accessed | tf_op | source)
XLA Modules:
  0.0 131.4 jit_solution(18264440401824441944)
XLA Ops:
  0.6 119.4 %mlp_backward.1.kept = bf16[4736,3584]{1,0:T(8,128)(2,1)S(1)} custom-call(bf16[2048,3584]{1,0:T(8,128)(2,1)} %x.1, bf16[2048,3584]{1,0:T(8,128)(2,1)} %dy.1, bf16[2048,896]{1,0:T(8,128)(2,1)} %gate.1, bf16[2048,896]{1,0:T(8,128)(2,1)} %up.1, bf16[3584,896]{1,0:T(8,128)(2,1)} %w_gate.1, bf16[3584,896]{1,0:T(8,128)(2,1)} %w_up.1, bf16[896,3584]{1,0:T(8,128)(2,1)} %w_down.1), custom_call_target="tpu_custom_call" | custom-call | tf_op jit(solution)/shard_map/mlp_backward/pallas_call | solution.py:347
  120.0 11.4 %writer.1 = (bf16[2048,3584]{1,0:T(8,128)(2,1)}, bf16[3584,896]{1,0:T(8,128)(2,1)}, bf16[3584,896]{1,0:T(8,128)(2,1)}, bf16[896,3584]{1,0:T(8,128)(2,1)}) custom-call(bf16[4736,3584]{1,0:T(8,128)(2,1)S(1)} %mlp_backward.1.kept), custom_call_target="tpu_custom_call" | custom-call | tf_op jit(solution)/shard_map/writer/pallas_call | solution.py:361

commit v3 on v2

--- a/solution.py
+++ b/solution.py
@@ -87,7 +87,6 @@
     barrier = pltpu.get_barrier_semaphore()
     for other in (*near, partner):
         pl.semaphore_signal(barrier, inc=1, device_id={"tp": other}, device_id_type=MESH)
-    pl.semaphore_wait(barrier, 4)
 
     def send(src, dst, stage, k, to):
         pltpu.make_async_remote_copy(src_ref=src, dst_ref=dst, send_sem=ssem.at[stage, k], recv_sem=rsem.at[stage, k],
@@ -216,9 +215,6 @@
         @pl.when(s == 0)
         def _():
             download.wait()
-            for pair in wloads:
-                for c in pair:
-                    c.start()
 
         for c in load_chunk(s, q, *bufs):
             c.wait()
@@ -257,6 +253,10 @@
     def phase1(*bufs):
         for c in load_chunk(0, 0, *bufs):
             c.start()
+        for pair in wloads:
+            for c in pair:
+                c.start()
+        pl.semaphore_wait(barrier, 4)
 
         def body(s, _):
             slot1(bufs, s)
@@ -327,7 +327,8 @@
 
 def writer(kept, dx, dwg, dwu, dwd, sem):
     rows, (dim, ff) = dx.shape[0], dwg.shape
-    pairs = [(kept.at[0:rows], dx), (kept.at[rows:rows + ff], dwd)]
+    pairs = [(kept.at[i * 256:(i + 1) * 256], dx.at[i * 256:(i + 1) * 256]) for i in range(rows // 256)]
+    pairs += [(kept.at[rows + i * 128:rows + (i + 1) * 128], dwd.at[i * 128:(i + 1) * 128]) for i in range(ff // 128)]
     for w, out in enumerate((dwg, dwu)):
         start = rows + (1 + w) * ff
         pairs += [(kept.at[start:start + ff, b * ff:(b + 1) * ff], out.at[b * ff:(b + 1) * ff]) for b in range(dim // ff)]
@@ -363,7 +364,7 @@
         out_shape=tuple(jax.ShapeDtypeStruct(g, BF) for g in ((rows, dim), (dim, ff), (dim, ff), (ff, dim))),
         in_specs=[inside],
         out_specs=(hbm,) * 4,
-        scratch_shapes=[dma((2 * n_blocks + 2,))],
+        scratch_shapes=[dma((2 * n_blocks + rows // 256 + ff // 128,))],
         compiler_params=pltpu.CompilerParams(vmem_limit_bytes=WRITER_LIMIT),
         name="writer",
     )(kept)

time: 132 us -> 130 us (0.985)
  no operation moved by 1% of the time
where the time goes in v3:
time: 130 us
  Pallas kernels  130 us (100%)
    pallas_call x1, Pallas kernels, backward(): pl.pallas_call(kernel, out_shape=vmem((rows + 3 * ff, dim), BF), in_specs...  118 us
    pallas_call x1, Pallas kernels, backward(): pl.pallas_call(writer, out_shape=tuple((jax.ShapeDtypeStruct(g, BF) for g...  11.2 us

profile of v3, /device:TPU:0, one launch (start us, length us, event | category | flops | bytes accessed | tf_op | source)
XLA Modules:
  0.0 130.3 jit_solution(6688830061636015375)
XLA Ops:
  0.6 118.4 %mlp_backward.1.kept = bf16[4736,3584]{1,0:T(8,128)(2,1)S(1)} custom-call(bf16[2048,3584]{1,0:T(8,128)(2,1)} %x.1, bf16[2048,3584]{1,0:T(8,128)(2,1)} %dy.1, bf16[2048,896]{1,0:T(8,128)(2,1)} %gate.1, bf16[2048,896]{1,0:T(8,128)(2,1)} %up.1, bf16[3584,896]{1,0:T(8,128)(2,1)} %w_gate.1, bf16[3584,896]{1,0:T(8,128)(2,1)} %w_up.1, bf16[896,3584]{1,0:T(8,128)(2,1)} %w_down.1), custom_call_target="tpu_custom_call" | custom-call | tf_op jit(solution)/shard_map/mlp_backward/pallas_call | solution.py:348
  119.1 11.2 %writer.1 = (bf16[2048,3584]{1,0:T(8,128)(2,1)}, bf16[3584,896]{1,0:T(8,128)(2,1)}, bf16[3584,896]{1,0:T(8,128)(2,1)}, bf16[896,3584]{1,0:T(8,128)(2,1)}) custom-call(bf16[4736,3584]{1,0:T(8,128)(2,1)S(1)} %mlp_backward.1.kept), custom_call_target="tpu_custom_call" | custom-call | tf_op jit(solution)/shard_map/writer/pallas_call | solution.py:362

commit v4 on v3

--- a/solution.py
+++ b/solution.py
@@ -180,14 +180,20 @@
     def stage5(k):
         gather(k, AG3, AG2, q2, 1)
 
+    def pass_on(k, ours):
+        for p in range(3):
+            cols, (b1, _, _), _ = geometry(p, k)
+            place = mine_at(k, q1 * b1 if ours else q1 * (1 - b1), q1)
+            send(kept.at[place, cols], kept.at[place, cols], DG, k, partner)
+
     def stage6(k):
         gather(k, AG2, AG1, q1, 0)
+        pl.semaphore_wait(credit, 1)
+        pass_on(k, True)
 
     def stage7(k):
         await_bytes(AG1, k, rsem)
-        pl.semaphore_wait(credit, 1)
-        place = mine_at(k, 0, HALF)
-        send(kept.at[place], kept.at[place], DG, k, partner)
+        pass_on(k, False)
 
     stages = (stage0, stage1, stage2, stage3, stage4, stage5, stage6, stage7)
 

time: 130 us -> 130 us (level)
  no operation moved by 1% of the time
where the time goes in v4:
time: 130 us
  Pallas kernels  129 us (99%)
    pallas_call x1, Pallas kernels, backward(): pl.pallas_call(kernel, out_shape=vmem((rows + 3 * ff, dim), BF), in_specs...  118 us
    pallas_call x1, Pallas kernels, backward(): pl.pallas_call(writer, out_shape=tuple((jax.ShapeDtypeStruct(g, BF) for g...  11.2 us

profile of v4, /device:TPU:0, one launch (start us, length us, event | category | flops | bytes accessed | tf_op | source)
XLA Modules:
  0.0 129.8 jit_solution(16332324401996231362)
XLA Ops:
  0.6 117.9 %mlp_backward.1.kept = bf16[4736,3584]{1,0:T(8,128)(2,1)S(1)} custom-call(bf16[2048,3584]{1,0:T(8,128)(2,1)} %x.1, bf16[2048,3584]{1,0:T(8,128)(2,1)} %dy.1, bf16[2048,896]{1,0:T(8,128)(2,1)} %gate.1, bf16[2048,896]{1,0:T(8,128)(2,1)} %up.1, bf16[3584,896]{1,0:T(8,128)(2,1)} %w_gate.1, bf16[3584,896]{1,0:T(8,128)(2,1)} %w_up.1, bf16[896,3584]{1,0:T(8,128)(2,1)} %w_down.1), custom_call_target="tpu_custom_call" | custom-call | tf_op jit(solution)/shard_map/mlp_backward/pallas_call | solution.py:354
  118.5 11.2 %writer.1 = (bf16[2048,3584]{1,0:T(8,128)(2,1)}, bf16[3584,896]{1,0:T(8,128)(2,1)}, bf16[3584,896]{1,0:T(8,128)(2,1)}, bf16[896,3584]{1,0:T(8,128)(2,1)}) custom-call(bf16[4736,3584]{1,0:T(8,128)(2,1)S(1)} %mlp_backward.1.kept), custom_call_target="tpu_custom_call" | custom-call | tf_op jit(solution)/shard_map/writer/pallas_call | solution.py:368

commit v5 on v4

--- a/solution.py
+++ b/solution.py
@@ -130,9 +130,13 @@
         a = lax.rem(k, SLOTS)
         for p in range(3):
             cols, (b1, _, _), (to, _, _) = geometry(p, k)
-            out, keep = q1 * (1 - b1), q1 * b1
+            out = q1 * (1 - b1)
             staged[a, 0:q1, cols] = (own[at(out, q1), cols] + kept[mine_at(k, out, q1), cols].astype(F32)).astype(BF)
             send(staged.at[a, 0:q1, cols], kept.at[spare_at(k, 0, q1), cols], RS1, k, to)
+
+        for p in range(3):
+            cols, (b1, _, _), _ = geometry(p, k)
+            keep = q1 * b1
             acc[a, :, cols] = own[at(keep, q1), cols] + kept[mine_at(k, keep, q1), cols].astype(F32)
 
     def stage2(k):
@@ -140,10 +144,14 @@
         a = lax.rem(k, SLOTS)
         for p in range(3):
             cols, (_, b2, _), (_, to, _) = geometry(p, k)
-            out, keep = q2 * (1 - b2), q2 * b2
+            out = q2 * (1 - b2)
             stage = slice(q1, q1 + q2)
             staged[a, stage, cols] = (acc[a, at(out, q2), cols] + kept[spare_at(k, out, q2), cols].astype(F32)).astype(BF)
             send(staged.at[a, stage, cols], kept.at[spare_at(k, q1, q2), cols], RS2, k, to)
+
+        for p in range(3):
+            cols, (_, b2, _), _ = geometry(p, k)
+            keep = q2 * b2
             acc[a, at(keep, q2), cols] = acc[a, at(keep, q2), cols] + kept[spare_at(k, keep, q2), cols].astype(F32)
 
     def stage3(k):
@@ -151,11 +159,15 @@
         a = lax.rem(k, SLOTS)
         for p in range(3):
             cols, (_, b2, b3), (_, _, to) = geometry(p, k)
-            out, keep = q3 * (1 - b3), q3 * b3
+            out = q3 * (1 - b3)
             stage = slice(q1 + q2, q1 + q2 + q3)
             staged[a, stage, cols] = (acc[a, at(q2 * b2 + out, q3), cols]
                                       + kept[spare_at(k, q1 + out, q3), cols].astype(F32)).astype(BF)
             send(staged.at[a, stage, cols], kept.at[spare_at(k, q1 + q2, q3), cols], RS3, k, to)
+
+        for p in range(3):
+            cols, (_, b2, b3), _ = geometry(p, k)
+            keep = q3 * b3
             place = at(q2 * b2 + keep, q3)
             acc[a, place, cols] = acc[a, place, cols] + kept[spare_at(k, q1 + keep, q3), cols].astype(F32)
 
@@ -247,8 +259,7 @@
         theirs = pl.ds(pl.multiple_of(base + HALF * (1 - core), HALF), HALF)
         mine = pl.ds(pl.multiple_of(base + HALF * core, HALF), HALF)
         lhs = jnp.concatenate([dgu[theirs], dgu[mine]], axis=0)
-        for n in range(2):
-            cols = slice(n * (dim // 2), (n + 1) * (dim // 2))
+        for cols in (slice(0, dim),):
             rhs = jnp.concatenate([weight(w, cols.start, cols.stop) for w in range(2)], axis=1)
             term = lax.dot_general(lhs, rhs, NT, preferred_element_type=F32)
             pbuf[:, cols] = term[:HALF].astype(BF)

time: 130 us -> 130 us (level)
  no operation moved by 1% of the time
where the time goes in v5:
time: 130 us
  Pallas kernels  129 us (99%)
    pallas_call x1, Pallas kernels, backward(): pl.pallas_call(kernel, out_shape=vmem((rows + 3 * ff, dim), BF), in_specs...  118 us
    pallas_call x1, Pallas kernels, backward(): pl.pallas_call(writer, out_shape=tuple((jax.ShapeDtypeStruct(g, BF) for g...  11.2 us

profile of v5, /device:TPU:0, one launch (start us, length us, event | category | flops | bytes accessed | tf_op | source)
XLA Modules:
  0.0 129.8 jit_solution(12098698168607546728)
XLA Ops:
  0.6 117.9 %mlp_backward.1.kept = bf16[4736,3584]{1,0:T(8,128)(2,1)S(1)} custom-call(bf16[2048,3584]{1,0:T(8,128)(2,1)} %x.1, bf16[2048,3584]{1,0:T(8,128)(2,1)} %dy.1, bf16[2048,896]{1,0:T(8,128)(2,1)} %gate.1, bf16[2048,896]{1,0:T(8,128)(2,1)} %up.1, bf16[3584,896]{1,0:T(8,128)(2,1)} %w_gate.1, bf16[3584,896]{1,0:T(8,128)(2,1)} %w_up.1, bf16[896,3584]{1,0:T(8,128)(2,1)} %w_down.1), custom_call_target="tpu_custom_call" | custom-call | tf_op jit(solution)/shard_map/mlp_backward/pallas_call | solution.py:365
  118.5 11.2 %writer.1 = (bf16[2048,3584]{1,0:T(8,128)(2,1)}, bf16[3584,896]{1,0:T(8,128)(2,1)}, bf16[3584,896]{1,0:T(8,128)(2,1)}, bf16[896,3584]{1,0:T(8,128)(2,1)}) custom-call(bf16[4736,3584]{1,0:T(8,128)(2,1)S(1)} %mlp_backward.1.kept), custom_call_target="tpu_custom_call" | custom-call | tf_op jit(solution)/shard_map/writer/pallas_call | solution.py:379
